TPU v7x, 32 devices: a whole 2x2x4 slice. The times are simulated.
32 devices in a mesh: dp: 16 (over z, y, core), tensor: 2 (over x).
Axes of the slice: x: 2, y: 2, z: 4, core: 2. Of those that a mesh axis runs over, the one named last changes fastest.
Arguments:
- tokens: bfloat16 [64, 144, 1024], P('dp', 'tensor'), may hold values from -150 to 150
- cotangent: bfloat16 [64, 144, 1024], P('dp', 'tensor'), may hold values from -6 to 6
- dispatch_weight: bfloat16 [1024, 32], replicated, may hold values from -3 to 3
- w_in: bfloat16 [32, 1024, 4096], P('dp', None, 'tensor'), may hold values from -0.1875 to 0.1875
- w_out: bfloat16 [32, 4096, 1024], P('dp', 'tensor'), may hold values from -0.09375 to 0.09375
Outputs:
- grad_tokens: bfloat16 [64, 144, 1024], P('dp', 'tensor')
- grad_router: float32 [1024, 32], replicated
- grad_w_in: bfloat16 [32, 1024, 4096], P('dp', None, 'tensor')
- grad_w_out: bfloat16 [32, 4096, 1024], P('dp', 'tensor')
All inputs are finite; a program needn't handle non-finite values.
Results may differ from a plain program's by a relative error of at most 0.0079.
Values may be sent and summed in bfloat16 or wider, within the bound.
A program may use at most 64 MiB of HBM per device.

v0:
```python
import jax
import jax.numpy as jnp
from jax import lax
from jax.sharding import PartitionSpec as P


def to_experts(partial_rows):
    shared_part = lax.psum_scatter(partial_rows, "tensor", scatter_dimension=2, tiled=True).astype(
        jnp.bfloat16
    )
    arrived = lax.all_to_all(shared_part, "dp", split_axis=1, concat_axis=0, tiled=True)
    result = lax.all_gather(arrived, "tensor", axis=2, tiled=True)
    return result


def to_images(partial_rows):
    shared_part = lax.psum_scatter(partial_rows, "tensor", scatter_dimension=2, tiled=True).astype(
        jnp.bfloat16
    )
    arrived = lax.all_to_all(shared_part, "dp", split_axis=0, concat_axis=1, tiled=True)
    result = lax.all_gather(arrived, "tensor", axis=2, tiled=True)
    return result


def dispatch_softmax(logits):
    local_max = jnp.max(logits, axis=1)
    global_max = lax.pmax(local_max, "tensor")
    exponent = jnp.exp(logits - global_max[:, None, :])
    totals = lax.psum(jnp.sum(exponent, axis=1), "tensor")
    return exponent / totals[:, None, :]


def on_device(tokens, cotangent, dispatch_weight, w_in, w_out):
    wide = jnp.float32
    logits = jnp.einsum("isd,de->ise", tokens, dispatch_weight, preferred_element_type=wide)
    dispatch = dispatch_softmax(logits)
    combine = jax.nn.softmax(logits, axis=2)
    dispatch_low = dispatch.astype(jnp.bfloat16)
    combine_low = combine.astype(jnp.bfloat16)
    slot_inputs = to_experts(
        jnp.einsum("ise,isd->ied", dispatch_low, tokens, preferred_element_type=wide)
    )
    pre_act = jnp.einsum("ied,edf->ief", slot_inputs, w_in, preferred_element_type=wide)
    hidden_act, gelu_back = jax.vjp(jax.nn.gelu, pre_act)
    hidden_low = hidden_act.astype(jnp.bfloat16)
    slot_outputs = to_images(
        jnp.einsum("ief,efd->ied", hidden_low, w_out, preferred_element_type=wide)
    )
    grad_combine = jnp.einsum("isd,ied->ise", cotangent, slot_outputs, preferred_element_type=wide)
    grad_slots_out = to_experts(
        jnp.einsum("ise,isd->ied", combine_low, cotangent, preferred_element_type=wide)
    )
    grad_hidden = jnp.einsum("ied,efd->ief", grad_slots_out, w_out, preferred_element_type=wide)
    grad_pre = gelu_back(grad_hidden)[0].astype(jnp.bfloat16)
    grad_w_out = jnp.einsum(
        "ief,ied->efd", hidden_low, grad_slots_out, preferred_element_type=wide
    ).astype(jnp.bfloat16)
    grad_w_in = jnp.einsum(
        "ied,ief->edf", slot_inputs, grad_pre, preferred_element_type=wide
    ).astype(jnp.bfloat16)
    grad_slots_in = to_images(
        jnp.einsum("ief,edf->ied", grad_pre, w_in, preferred_element_type=wide)
    )
    grad_dispatch = jnp.einsum("isd,ied->ise", tokens, grad_slots_in, preferred_element_type=wide)
    column_dot = lax.psum(jnp.sum(grad_dispatch * dispatch, axis=1), "tensor")
    row_dot = jnp.sum(grad_combine * combine, axis=2, keepdims=True)
    grad_logits = (
        combine * (grad_combine - row_dot) + dispatch * (grad_dispatch - column_dot[:, None, :])
    ).astype(jnp.bfloat16)
    token_part = jnp.einsum(
        "ise,ied->isd", dispatch_low, grad_slots_in, preferred_element_type=wide
    )
    router_part = jnp.einsum(
        "ise,de->isd", grad_logits, dispatch_weight, preferred_element_type=wide
    )
    grad_tokens = (token_part + router_part).astype(jnp.bfloat16)
    local_router = jnp.einsum("isd,ise->de", tokens, grad_logits, preferred_element_type=wide)
    grad_router = lax.psum(local_router, ("dp", "tensor"))
    return (grad_tokens, grad_router, grad_w_in, grad_w_out)


def solution(mesh):
    return jax.shard_map(
        on_device,
        mesh=mesh,
        in_specs=(
            P("dp", "tensor", None),
            P("dp", "tensor", None),
            P(),
            P("dp", None, "tensor"),
            P("dp", "tensor", None),
        ),
        out_specs=(P("dp", "tensor", None), P(), P("dp", None, "tensor"), P("dp", "tensor", None)),
        check_vma=False,
    )
```

profile of v0, /device:TPU:0, one launch (start us, length us, event | category | flops | bytes accessed | tf_op | source)
XLA Modules:
  0.0 270.4 jit_solution(4491643558524088509)
XLA Ops:
  7.2 1.0 copy-done
  8.2 1.3 fusion.37
  9.5 0.2 fusion.38
  9.7 2.1 fusion.26
  11.8 0.0 reduce-scatter.7.cloned.1.call-start
  11.9 5.9 %pmax.7 = f32[4,32]{1,0:T(4,128)S(1)} all-reduce(f32[4,32]{1,0:T(4,128)S(1)} %get-tuple-element.4), channel_id=1, replica_groups=mesh['dp'=16,'tensor'=2] {'tensor'}, use_global_device_ids=true, to_apply=%region_1.0 | all-reduce | flops 128 | bytes 1024 | tf_op jit(solution)/shard_map/pmax | solution.py:27
  17.7 0.2 fusion.25
  17.9 4.9 %psum.21 = f32[4,32]{1,0:T(4,128)S(1)} all-reduce(f32[4,32]{1,0:T(4,128)S(1)} %fusion.25), channel_id=1, replica_groups=mesh['dp'=16,'tensor'=2] {'tensor'}, use_global_device_ids=true, to_apply=%region_3.0 | all-reduce | flops 128 | bytes 1024 | tf_op jit(solution)/shard_map/psum | solution.py:29
  22.9 1.1 fusion.29
  24.0 5.4 %reduce-scatter.5.cloned.1.call-done = f32[4,32,512]{2,1,0:T(8,128)} async-done(((f32[4,32,1024]{2,1,0:T(8,128)}), f32[4,32,512]{2,1,0:T(8,128)}) %reduce-scatter.5.cloned.1.call-update) | async-done | bytes 262160 | tf_op jit(solution)/shard_map/reduce_scatter | solution.py:8
  29.4 1.0 convert_element_type.38
  30.3 0.8 copy.13
  31.1 5.6 %all-to-all-start = ((bf16[4,32,512]{2,0,1:T(4,128)(2,1)}), bf16[4,32,512]{2,0,1:T(4,128)(2,1)S(1)}, u32[]{:S(2)}, u32[]{:S(2)}) async-start(bf16[4,32,512]{2,0,1:T(4,128)(2,1)} %copy.13), calls=%async_computation.1 | async-start | bytes 262144 | tf_op jit(solution)/shard_map/all_to_all | solution.py:11
  36.7 10.1 %reduce-scatter.7.cloned.1.call-done = f32[4,32,512]{2,1,0:T(8,128)} async-done(((f32[4,32,1024]{2,1,0:T(8,128)}), f32[4,32,512]{2,1,0:T(8,128)}) %reduce-scatter.7.cloned.1.call-update) | async-done | bytes 262160 | tf_op jit(solution)/shard_map/reduce_scatter | solution.py:8
  46.9 1.0 convert_element_type.39
  47.8 0.8 copy.15
  48.6 5.6 %all-to-all-start.1 = ((bf16[4,32,512]{2,0,1:T(4,128)(2,1)}), bf16[4,32,512]{2,0,1:T(4,128)(2,1)S(1)}, u32[]{:S(2)}, u32[]{:S(2)}) async-start(bf16[4,32,512]{2,0,1:T(4,128)(2,1)} %copy.15), calls=%async_computation.3 | async-start | bytes 262144 | tf_op jit(solution)/shard_map/all_to_all | solution.py:11
  54.4 6.5 %all_gather.12 = bf16[64,2,1024]{2,0,1:T(8,128)(2,1)S(1)} all-gather(bf16[64,2,512]{2,0,1:T(8,128)(2,1)S(1)} %all_to_all.55), channel_id=1, replica_groups=mesh['dp'=16,'tensor'=2] {'tensor'}, dimensions={2}, use_global_device_ids=true | all-gather | bytes 393216 | tf_op jit(solution)/shard_map/all_gather | solution.py:12
  60.8 1.3 all-to-all-done.1
  62.2 5.8 %all_gather.13 = bf16[64,2,1024]{2,0,1:T(8,128)(2,1)S(1)} all-gather(bf16[64,2,512]{2,0,1:T(8,128)(2,1)S(1)} %all_to_all.59), channel_id=1, replica_groups=mesh['dp'=16,'tensor'=2] {'tensor'}, dimensions={2}, use_global_device_ids=true | all-gather | bytes 393216 | tf_op jit(solution)/shard_map/all_gather | solution.py:12
  68.0 5.1 %convolution_bitcast_fusion = f32[64,2,2048]{2,0,1:T(8,128)S(1)} fusion(bf16[64,2,1024]{2,0,1:T(8,128)(2,1)S(1)} %all_gather.13, bf16[2,1024,2048]{2,1,0:T(8,128)(2,1)} %param.8), kind=kOutput, calls=%fused_computation.4 | convolution fusion | flops 536870912 | bytes 9699328 | tf_op jit(solution)/shard_map/ied,edf->ief/dot_general | solution.py:43
  73.1 2.9 %fusion.16 = bf16[64,2,2048]{2,0,1:T(8,128)(2,1)S(1)} fusion(f32[64,2,2048]{2,0,1:T(8,128)S(1)} %convolution_bitcast_fusion, bf16[64,2,1024]{2,0,1:T(8,128)(2,1)S(1)} %all_gather.12, bf16[2,2048,1024]{2,1,0:T(8,128)(2,1)S(1)} %copy-done.1), kind=kOutput, calls=%fused_computation.28 | convolution fusion | flops 542113792 | bytes 10223616 | tf_op jit(solution)/shard_map/ied,efd->ief/dot_general | solution.py:53
  76.0 3.5 %convolution_bitcast_fusion.3 = f32[64,2,1024]{2,0,1:T(8,128)} fusion(bf16[64,2,2048]{2,0,1:T(8,128)(2,1)S(1)} %fusion.16, bf16[2,1024,2048]{2,1,0:T(8,128)(2,1)S(1)} %bitcast.67), kind=kOutput, calls=%fused_computation.11 | convolution fusion | flops 536870912 | bytes 9437184 | tf_op jit(solution)/shard_map/ief,edf->ied/dot_general | solution.py:62
  79.6 5.7 %convolution_bitcast_fusion.2 = f32[64,2,1024]{2,0,1:T(8,128)} fusion(bf16[2,2048,1024]{2,1,0:T(8,128)(2,1)} %param.9, f32[64,2,2048]{2,0,1:T(8,128)S(1)} %convolution_bitcast_fusion), kind=kOutput, calls=%fused_computation.10 | convolution fusion | flops 539230208 | bytes 9961472 | tf_op jit(solution)/shard_map/ief,efd->ied/dot_general | solution.py:47
  85.3 5.8 %convolution_convert_fusion = bf16[2,2048,1024]{2,1,0:T(8,128)(2,1)} fusion(bf16[64,2,1024]{2,0,1:T(8,128)(2,1)S(1)} %all_gather.12, f32[64,2,2048]{2,0,1:T(8,128)S(1)} %convolution_bitcast_fusion), kind=kOutput, calls=%fused_computation.2 | convolution fusion | flops 543424512 | bytes 9699328 | tf_op jit(solution)/shard_map/ief,ied->efd/dot_general | solution.py:55
  91.1 2.0 reduce-scatter.9.cloned.1.call-done
  93.1 1.0 convert_element_type.41
  94.1 0.8 copy.17
  94.9 5.6 %all-to-all-start.2 = ((bf16[64,2,512]{2,1,0:T(2,128)(2,1)}), bf16[64,2,512]{2,1,0:T(2,128)(2,1)S(1)}, u32[]{:S(2)}, u32[]{:S(2)}) async-start(bf16[64,2,512]{2,1,0:T(2,128)(2,1)} %copy.17), calls=%async_computation.5 | async-start | bytes 262144 | tf_op jit(solution)/shard_map/all_to_all | solution.py:20
  100.5 5.8 %convolution_convert_fusion.1 = bf16[2,1024,2048]{2,1,0:T(8,128)(2,1)} fusion(bf16[64,2,1024]{2,0,1:T(8,128)(2,1)S(1)} %all_gather.13, bf16[64,2,2048]{2,0,1:T(8,128)(2,1)S(1)} %fusion.16), kind=kOutput, calls=%fused_computation.3 | convolution fusion | flops 541065216 | bytes 9175040 | tf_op jit(solution)/shard_map/ied,ief->edf/dot_general | solution.py:58
  106.3 4.2 %reduce-scatter.11.cloned.1.call-done = f32[64,2,512]{2,0,1:T(8,128)} async-done(((f32[64,2,1024]{2,0,1:T(8,128)}), f32[64,2,512]{2,0,1:T(8,128)}) %reduce-scatter.11.cloned.1.call-update) | async-done | bytes 262160 | tf_op jit(solution)/shard_map/reduce_scatter | solution.py:17
  110.4 1.0 convert_element_type.43
  111.4 0.8 copy.19
  112.2 5.6 %all-to-all-start.3 = ((bf16[64,2,512]{2,1,0:T(2,128)(2,1)}), bf16[64,2,512]{2,1,0:T(2,128)(2,1)S(1)}, u32[]{:S(2)}, u32[]{:S(2)}) async-start(bf16[64,2,512]{2,1,0:T(2,128)(2,1)} %copy.19), calls=%async_computation.7 | async-start | bytes 262144 | tf_op jit(solution)/shard_map/all_to_all | solution.py:20
  117.9 0.1 copy.26
  118.0 0.1 all_to_all.63
  118.1 6.5 %all_gather.14 = bf16[4,32,1024]{2,1,0:T(8,128)(2,1)S(1)} all-gather(bf16[4,32,512]{2,1,0:T(8,128)(2,1)S(1)} %all_to_all.63), channel_id=1, replica_groups=mesh['dp'=16,'tensor'=2] {'tensor'}, dimensions={2}, use_global_device_ids=true | all-gather | bytes 393216 | tf_op jit(solution)/shard_map/all_gather | solution.py:21
  124.5 0.4 multiply_reduce_fusion.1
  124.9 4.9 %psum.22 = f32[4,32]{1,0:T(4,128)S(1)} all-reduce(f32[4,32]{1,0:T(4,128)S(1)} %get-tuple-element.8), channel_id=1, replica_groups=mesh['dp'=16,'tensor'=2] {'tensor'}, use_global_device_ids=true, to_apply=%region_12.0 | all-reduce | flops 128 | bytes 1024 | tf_op jit(solution)/shard_map/psum | solution.py:65
  129.9 0.1 copy.25
  129.9 0.1 all_to_all.67
  130.0 5.6 %all_gather.15 = bf16[4,32,1024]{2,1,0:T(8,128)(2,1)S(1)} all-gather(bf16[4,32,512]{2,1,0:T(8,128)(2,1)S(1)} %all_to_all.67), channel_id=1, replica_groups=mesh['dp'=16,'tensor'=2] {'tensor'}, dimensions={2}, use_global_device_ids=true | all-gather | bytes 393216 | tf_op jit(solution)/shard_map/all_gather | solution.py:21
  135.7 0.3 convolution_bitcast_fusion.6
  135.9 1.0 convolution_bitcast_fusion.4
  137.0 0.4 fusion.9
  137.5 1.3 fusion.2
  138.7 123.5 %all-reduce.2.cloned.1.call-done = f32[1024,32]{0,1:T(8,128)} async-done(((f32[1024,32]{0,1:T(8,128)}), f32[1024,32]{0,1:T(8,128)}) %all-reduce.2.cloned.1.call-update) | async-done | bytes 131088 | tf_op jit(solution)/shard_map/psum | solution.py:78
  262.3 1.6 copy.30
  (28 shorter events, 0.5 us)
Async XLA Ops:
  7.2 1.1 copy-start
  7.2 22.2 %reduce-scatter.5.cloned.1.call-start = ((), (), s32[]{:S(2)}) async-start(), calls=%async_computation.8 | async-start | bytes 786432 | tf_op jit(solution)/shard_map/reduce_scatter | solution.py:8
  11.8 35.0 %reduce-scatter.7.cloned.1.call-start = ((), (), s32[]{:S(2)}) async-start(), calls=%async_computation.9 | async-start | bytes 786432 | tf_op jit(solution)/shard_map/reduce_scatter | solution.py:8
  31.1 17.5 %all-to-all-start = ((bf16[4,32,512]{2,0,1:T(4,128)(2,1)}), bf16[4,32,512]{2,0,1:T(4,128)(2,1)S(1)}, u32[]{:S(2)}, u32[]{:S(2)}) async-start(bf16[4,32,512]{2,0,1:T(4,128)(2,1)} %copy.13), calls=%async_computation.1 | async-start | bytes 262144 | tf_op jit(solution)/shard_map/all_to_all | solution.py:11
  48.6 13.5 %all-to-all-start.1 = ((bf16[4,32,512]{2,0,1:T(4,128)(2,1)}), bf16[4,32,512]{2,0,1:T(4,128)(2,1)S(1)}, u32[]{:S(2)}, u32[]{:S(2)}) async-start(bf16[4,32,512]{2,0,1:T(4,128)(2,1)} %copy.15), calls=%async_computation.3 | async-start | bytes 262144 | tf_op jit(solution)/shard_map/all_to_all | solution.py:11
  54.2 38.9 %reduce-scatter.9.cloned.1.call-start = ((), (), s32[]{:S(2)}) async-start(), calls=%async_computation.10 | async-start | bytes 786432 | tf_op jit(solution)/shard_map/reduce_scatter | solution.py:17
  62.2 10.9 %copy-start.1 = (bf16[2,2048,1024]{2,1,0:T(8,128)(2,1)S(1)}, bf16[2,2048,1024]{2,1,0:T(8,128)(2,1)}, u32[]{:S(2)}) copy-start(bf16[2,2048,1024]{2,1,0:T(8,128)(2,1)} %param.9) | copy-start | bytes 25165828
  62.2 13.8 %slice-start = ((s8[8388608]{0:T(1024)(128)(4,1)}), s8[4194304]{0:T(1024)(128)(4,1)S(1)}, s32[]{:S(2)}) async-start(s8[8388608]{0:T(1024)(128)(4,1)} %bitcast.66), calls=%async_computation.13 | async-start | bytes 8388608
  68.0 8.0 %slice-start.1 = ((s8[8388608]{0:T(1024)(128)(4,1)}), s8[4194304]{0:T(1024)(128)(4,1)S(1)}, s32[]{:S(2)}) async-start(s8[8388608]{0:T(1024)(128)(4,1)} %bitcast.66), calls=%async_computation.14 | async-start | bytes 8388608
  79.5 30.9 %reduce-scatter.11.cloned.1.call-start = ((), (), s32[]{:S(2)}) async-start(), calls=%async_computation.11 | async-start | bytes 786432 | tf_op jit(solution)/shard_map/reduce_scatter | solution.py:17
  91.1 44.6 %copy-start.2 = (bf16[4,72,1024]{2,1,0:T(8,128)(2,1)S(1)}, bf16[4,72,1024]{2,1,0:T(8,128)(2,1)}, u32[]{:S(2)}) copy-start(bf16[4,72,1024]{2,1,0:T(8,128)(2,1)} %param.6) | copy-start | bytes 1769476
  91.1 45.9 %copy-start.3 = (bf16[1024,32]{0,1:T(8,128)(2,1)S(1)}, bf16[1024,32]{0,1:T(8,128)(2,1)}, u32[]{:S(2)}) copy-start(bf16[1024,32]{0,1:T(8,128)(2,1)} %param.7) | copy-start | bytes 196612
  94.9 17.3 %all-to-all-start.2 = ((bf16[64,2,512]{2,1,0:T(2,128)(2,1)}), bf16[64,2,512]{2,1,0:T(2,128)(2,1)S(1)}, u32[]{:S(2)}, u32[]{:S(2)}) async-start(bf16[64,2,512]{2,1,0:T(2,128)(2,1)} %copy.17), calls=%async_computation.5 | async-start | bytes 262144 | tf_op jit(solution)/shard_map/all_to_all | solution.py:20
  112.2 17.6 %all-to-all-start.3 = ((bf16[64,2,512]{2,1,0:T(2,128)(2,1)}), bf16[64,2,512]{2,1,0:T(2,128)(2,1)S(1)}, u32[]{:S(2)}, u32[]{:S(2)}) async-start(bf16[64,2,512]{2,1,0:T(2,128)(2,1)} %copy.19), calls=%async_computation.7 | async-start | bytes 262144 | tf_op jit(solution)/shard_map/all_to_all | solution.py:20
  117.9 144.4 %all-reduce.2.cloned.1.call-start = ((), (), s32[]{:S(2)}) async-start(), calls=%async_computation.12 | async-start | bytes 262144 | tf_op jit(solution)/shard_map/psum | solution.py:78
Sparse Core Ops, SparseCore 0:
  11.9 17.3 reduce-scatter.4
  32.2 14.6 reduce-scatter.6
  79.6 13.4 reduce-scatter.8
  95.8 14.6 reduce-scatter.10
  137.6 124.6 all-reduce.1
where the time goes:
time: 271 us; the launch traced here: 270 us
  waiting for transfers between devices  147 us (54%)
  blocking collectives  40.1 us (15%)
  matrix products  36.6 us (14%)
  starting transfers between devices  22.7 us (8%)
  between operations  14 us (5%)
  local copies, waits for them, and re-layouts  6.18 us (2%)
  other arithmetic  4.2 us (2%)
    psum x1, waiting for transfers between devices, on_device(): grad_router = lax.psum(local_router, ('dp', 'tensor'))  124 us
    reduce_scatter x2, waiting for transfers between devices, to_experts(): lax.psum_scatter(partial_rows, 'tensor', scatter_dimension=2, tiled=True)  15.5 us
    all_gather x2, blocking collectives, to_experts(): result = lax.all_gather(arrived, 'tensor', axis=2, tiled=True)  12.2 us
    all_gather x2, blocking collectives, to_images(): result = lax.all_gather(arrived, 'tensor', axis=2, tiled=True)  12.1 us
    all_to_all x2, starting transfers between devices, to_images(): lax.all_to_all(shared_part, 'dp', split_axis=0, concat_axis=1, tiled=True)  11.3 us
    all_to_all x2, starting transfers between devices, to_experts(): lax.all_to_all(shared_part, 'dp', split_axis=1, concat_axis=0, tiled=True)  11.2 us
    reduce_scatter x2, waiting for transfers between devices, to_images(): lax.psum_scatter(partial_rows, 'tensor', scatter_dimension=2, tiled=True)  6.15 us
    pmax x1, blocking collectives, dispatch_softmax(): global_max = lax.pmax(local_max, 'tensor')  5.87 us
  transfers between devices with their start and end apart: 9, of which 6 were waited for; matrix products, arithmetic and copies ran while one was open for 10% of the time, Pallas kernels for 0%

commit v1 on v0

v1 whole, which is shorter than its diff:
```python
import functools

import jax
import jax.numpy as jnp
from jax import lax
from jax.experimental import pallas as pl
from jax.experimental.pallas import tpu as pltpu
from jax.sharding import PartitionSpec as P

MESH = pl.DeviceIdType.MESH


def exchange_kernel(
    groups, shards, x_ref, out_ref, arrived, summed,
    near_send, near_recv, far_send, far_recv, pass_send, pass_recv,
):
    me = lax.axis_index("dp")
    part = lax.axis_index("tensor")

    def group_at(offset):
        return lax.rem(me + offset, groups)

    def shard_at(offset):
        return lax.rem(part + offset, shards)

    barrier = pltpu.get_barrier_semaphore()
    for k in range(1, shards):
        pl.semaphore_signal(barrier, inc=1, device_id=(me, shard_at(k)), device_id_type=MESH)

    def greet(o, carry):
        pl.semaphore_signal(barrier, inc=1, device_id=(group_at(o), part), device_id_type=MESH)
        return carry

    lax.fori_loop(1, groups, greet, 0)
    pl.semaphore_wait(barrier, shards - 1 + groups - 1)

    def near(k, o):
        return pltpu.make_async_remote_copy(
            src_ref=x_ref.at[shard_at(k), group_at(o)],
            dst_ref=arrived.at[k - 1, o],
            send_sem=near_send.at[k - 1, o],
            recv_sem=near_recv.at[k - 1, o],
            device_id=(me, shard_at(k)),
            device_id_type=MESH,
        )

    def far(o):
        return pltpu.make_async_remote_copy(
            src_ref=summed.at[o],
            dst_ref=out_ref.at[part, me],
            send_sem=far_send.at[o],
            recv_sem=far_recv.at[o],
            device_id=(group_at(o), part),
            device_id_type=MESH,
        )

    def passed(k, o):
        source = group_at(groups - o)
        return pltpu.make_async_remote_copy(
            src_ref=out_ref.at[part, source],
            dst_ref=out_ref.at[part, source],
            send_sem=pass_send.at[k - 1, o],
            recv_sem=pass_recv.at[k - 1, o],
            device_id=(me, shard_at(k)),
            device_id_type=MESH,
        )

    def add_up(o):
        total = x_ref[part, group_at(o)].astype(jnp.float32)
        for k in range(1, shards):
            near(k, o).wait_recv()
            total = total + arrived[k - 1, o].astype(jnp.float32)
        return total.astype(out_ref.dtype)

    def send_near(o, carry):
        for k in range(1, shards):
            near(k, lax.rem(o, groups)).start()
        return carry

    lax.fori_loop(1, groups + 1, send_near, 0)

    def send_far(o, carry):
        summed[o] = add_up(o)
        far(o).start()
        return carry

    lax.fori_loop(1, groups, send_far, 0)
    out_ref[part, me] = add_up(0)
    for k in range(1, shards):
        passed(k, 0).start()

    def pass_on(o, carry):
        far(o).wait_recv()
        for k in range(1, shards):
            passed(k, o).start()
        return carry

    lax.fori_loop(1, groups, pass_on, 0)

    def finish(o, carry):
        for k in range(1, shards):
            near(k, o).wait_send()
            passed(k, o).wait_send()
            passed(k, o).wait_recv()
        return carry

    lax.fori_loop(0, groups, finish, 0)

    def finish_far(o, carry):
        far(o).wait_send()
        return carry

    lax.fori_loop(1, groups, finish_far, 0)


def exchange(x, collective_id):
    shards, groups, rows, columns = x.shape
    vmem = pl.BlockSpec(memory_space=pltpu.VMEM)
    near_shape = (max(shards - 1, 1), groups)
    return pl.pallas_call(
        functools.partial(exchange_kernel, groups, shards),
        out_shape=jax.ShapeDtypeStruct(x.shape, x.dtype),
        in_specs=[vmem],
        out_specs=vmem,
        scratch_shapes=[
            pltpu.VMEM(near_shape + (rows, columns), x.dtype),
            pltpu.VMEM((groups, rows, columns), x.dtype),
            pltpu.SemaphoreType.DMA(near_shape),
            pltpu.SemaphoreType.DMA(near_shape),
            pltpu.SemaphoreType.DMA((groups,)),
            pltpu.SemaphoreType.DMA((groups,)),
            pltpu.SemaphoreType.DMA(near_shape),
            pltpu.SemaphoreType.DMA(near_shape),
        ],
        compiler_params=pltpu.CompilerParams(collective_id=collective_id, has_side_effects=True),
        name=f"exchange_{collective_id}",
    )(x)


def total_kernel(groups, shards, x_ref, out_ref, arrived, send, recv, back_send, back_recv):
    devices = groups * shards
    me = lax.axis_index("dp") * shards + lax.axis_index("tensor")

    def target(o):
        to = lax.rem(me + o, devices)
        return to, (to // shards, lax.rem(to, shards))

    barrier = pltpu.get_barrier_semaphore()

    def greet(o, carry):
        pl.semaphore_signal(barrier, inc=1, device_id=target(o)[1], device_id_type=MESH)
        return carry

    lax.fori_loop(1, devices, greet, 0)
    pl.semaphore_wait(barrier, devices - 1)

    def out_copy(o):
        to, place = target(o)
        return pltpu.make_async_remote_copy(
            src_ref=x_ref.at[to],
            dst_ref=arrived.at[o],
            send_sem=send.at[o],
            recv_sem=recv.at[o],
            device_id=place,
            device_id_type=MESH,
        )

    def back_copy(o):
        return pltpu.make_async_remote_copy(
            src_ref=out_ref.at[me],
            dst_ref=out_ref.at[me],
            send_sem=back_send.at[o],
            recv_sem=back_recv.at[o],
            device_id=target(o)[1],
            device_id_type=MESH,
        )

    def begin(o, carry):
        out_copy(o).start()
        return carry

    lax.fori_loop(1, devices, begin, 0)

    def add(o, total):
        out_copy(o).wait_recv()
        return total + arrived[o]

    out_ref[me] = lax.fori_loop(1, devices, add, x_ref[me])

    def give(o, carry):
        back_copy(o).start()
        return carry

    lax.fori_loop(1, devices, give, 0)

    def finish(o, carry):
        out_copy(o).wait_send()
        back_copy(o).wait_send()
        back_copy(o).wait_recv()
        return carry

    lax.fori_loop(1, devices, finish, 0)


def total_over_mesh(x, groups, shards, collective_id):
    devices = groups * shards
    blocks = x.reshape(devices, -1, 128)
    vmem = pl.BlockSpec(memory_space=pltpu.VMEM)
    out = pl.pallas_call(
        functools.partial(total_kernel, groups, shards),
        out_shape=jax.ShapeDtypeStruct(blocks.shape, blocks.dtype),
        in_specs=[vmem],
        out_specs=vmem,
        scratch_shapes=[
            pltpu.VMEM(blocks.shape, blocks.dtype),
            pltpu.SemaphoreType.DMA((devices,)),
            pltpu.SemaphoreType.DMA((devices,)),
            pltpu.SemaphoreType.DMA((devices,)),
            pltpu.SemaphoreType.DMA((devices,)),
        ],
        compiler_params=pltpu.CompilerParams(collective_id=collective_id, has_side_effects=True),
        name="router_total",
    )(blocks)
    return out.reshape(x.shape)


def to_experts(rows, groups, shards, collective_id):
    count = len(rows)
    images, experts, width = rows[0].shape
    own, columns = experts // groups, width // shards
    x = jnp.stack([r.astype(jnp.bfloat16) for r in rows])
    x = x.reshape(count, images, groups, own, shards, columns)
    x = x.transpose(4, 2, 0, 3, 1, 5).reshape(shards, groups, -1, columns)
    y = exchange(x, collective_id).reshape(shards, groups, count, own, images, columns)
    y = y.transpose(2, 3, 1, 4, 0, 5).reshape(count, own, groups * images, width)
    return [y[k] for k in range(count)]


def to_images(rows, groups, shards, collective_id):
    count = len(rows)
    own, everyone, width = rows[0].shape
    images, columns = everyone // groups, width // shards
    x = jnp.stack([r.astype(jnp.bfloat16) for r in rows])
    x = x.reshape(count, own, groups, images, shards, columns)
    x = x.transpose(4, 2, 0, 3, 1, 5).reshape(shards, groups, -1, columns)
    y = exchange(x, collective_id).reshape(shards, groups, count, images, own, columns)
    y = y.transpose(2, 3, 1, 4, 0, 5).reshape(count, images, groups * own, width)
    return [y[k] for k in range(count)]


def dispatch_softmax(logits):
    local_max = jnp.max(logits, axis=1)
    local_sum = jnp.sum(jnp.exp(logits - local_max[:, None, :]), axis=1)
    both = lax.all_gather(jnp.stack([local_max, local_sum]), "tensor")
    global_max = jnp.max(both[:, 0], axis=0)
    totals = jnp.sum(both[:, 1] * jnp.exp(both[:, 0] - global_max), axis=0)
    return jnp.exp(logits - global_max[:, None, :]) / totals[:, None, :]


def on_device(groups, shards, tokens, cotangent, dispatch_weight, w_in, w_out):
    wide = jnp.float32
    logits = jnp.einsum("isd,de->ise", tokens, dispatch_weight, preferred_element_type=wide)
    dispatch = dispatch_softmax(logits)
    combine = jax.nn.softmax(logits, axis=2)
    dispatch_low = dispatch.astype(jnp.bfloat16)
    combine_low = combine.astype(jnp.bfloat16)
    slot_inputs, grad_slots_out = to_experts(
        [
            jnp.einsum("ise,isd->ied", dispatch_low, tokens, preferred_element_type=wide),
            jnp.einsum("ise,isd->ied", combine_low, cotangent, preferred_element_type=wide),
        ],
        groups, shards, 0,
    )
    pre_act = jnp.einsum("eid,edf->eif", slot_inputs, w_in, preferred_element_type=wide)
    hidden_act, gelu_back = jax.vjp(jax.nn.gelu, pre_act)
    hidden_low = hidden_act.astype(jnp.bfloat16)
    grad_hidden = jnp.einsum("eid,efd->eif", grad_slots_out, w_out, preferred_element_type=wide)
    grad_pre = gelu_back(grad_hidden)[0].astype(jnp.bfloat16)
    slot_outputs, grad_slots_in = to_images(
        [
            jnp.einsum("eif,efd->eid", hidden_low, w_out, preferred_element_type=wide),
            jnp.einsum("eif,edf->eid", grad_pre, w_in, preferred_element_type=wide),
        ],
        groups, shards, 1,
    )
    grad_w_out = jnp.einsum(
        "eif,eid->efd", hidden_low, grad_slots_out, preferred_element_type=wide
    ).astype(jnp.bfloat16)
    grad_w_in = jnp.einsum(
        "eid,eif->edf", slot_inputs, grad_pre, preferred_element_type=wide
    ).astype(jnp.bfloat16)
    grad_combine = jnp.einsum("isd,ied->ise", cotangent, slot_outputs, preferred_element_type=wide)
    grad_dispatch = jnp.einsum("isd,ied->ise", tokens, grad_slots_in, preferred_element_type=wide)
    column_dot = lax.psum(jnp.sum(grad_dispatch * dispatch, axis=1), "tensor")
    row_dot = jnp.sum(grad_combine * combine, axis=2, keepdims=True)
    grad_logits = (
        combine * (grad_combine - row_dot) + dispatch * (grad_dispatch - column_dot[:, None, :])
    ).astype(jnp.bfloat16)
    token_part = jnp.einsum(
        "ise,ied->isd", dispatch_low, grad_slots_in, preferred_element_type=wide
    )
    router_part = jnp.einsum(
        "ise,de->isd", grad_logits, dispatch_weight, preferred_element_type=wide
    )
    grad_tokens = (token_part + router_part).astype(jnp.bfloat16)
    local_router = jnp.einsum("isd,ise->ed", tokens, grad_logits, preferred_element_type=wide)
    grad_router = total_over_mesh(local_router, groups, shards, 2).T
    return (grad_tokens, grad_router, grad_w_in, grad_w_out)


def solution(mesh):
    return jax.shard_map(
        functools.partial(on_device, mesh.shape["dp"], mesh.shape["tensor"]),
        mesh=mesh,
        in_specs=(
            P("dp", "tensor", None),
            P("dp", "tensor", None),
            P(),
            P("dp", None, "tensor"),
            P("dp", "tensor", None),
        ),
        out_specs=(P("dp", "tensor", None), P(), P("dp", None, "tensor"), P("dp", "tensor", None)),
        check_vma=False,
    )
```

time: 271 us -> 125 us (0.46)
  waiting for transfers between devices: 147 us -> 0 us
  Pallas kernels: 0 us -> 59.7 us
  blocking collectives: 40.1 us -> 10.4 us
  starting transfers between devices: 22.7 us -> 0 us
  between operations: 14 us -> 0.99 us
  local copies, waits for them, and re-layouts: 6.18 us -> 11.8 us
  matrix products: 36.6 us -> 39.8 us
  other arithmetic: 4.2 us -> 1.39 us
    psum x1 -> x0, waiting for transfers between devices: 124 us -> none  [on_device(): grad_router = lax.psum(local_router, ('dp', 'tensor'))]
    pallas_call x0 -> x3, Pallas kernels: none -> 59.7 us  [the longest x2 42.7 us: exchange(): pl.pallas_call(functools.partial(exchange_kernel, groups, shards), out_sh...]
    all_to_all x4 -> x0, starting transfers between devices: 22.5 us -> none  [the longest x2 11.3 us: to_images(): lax.all_to_all(shared_part, 'dp', split_axis=0, concat_axis=1, tiled=True)]
    reduce_scatter x4 -> x0, waiting for transfers between devices: 21.7 us -> none  [the longest x2 15.5 us: to_experts(): lax.psum_scatter(partial_rows, 'tensor', scatter_dimension=2, tiled=True)]
    all_gather x4 -> x1, blocking collectives: 24.3 us -> 5.29 us  [dispatch_softmax(): both = lax.all_gather(jnp.stack([local_max, local_sum]), 'tensor')]
    pmax x1 -> x0, blocking collectives: 5.87 us -> none  [dispatch_softmax(): global_max = lax.pmax(local_max, 'tensor')]
    psum x1 -> x0, blocking collectives: 4.95 us -> none  [dispatch_softmax(): totals = lax.psum(jnp.sum(exponent, axis=1), 'tensor')]
    reshape x0 -> x4, local copies, waits for them, and re-layouts: none -> 4.31 us  [the longest x1 1.24 us: to_images(): exchange(x, collective_id)]
  transfers between devices with their start and end apart: 9 -> 0, of which waited for: 6 -> 0; matrix products, arithmetic and copies ran while one was open for 10% -> 0% of each run, Pallas kernels for 0% -> 0%
where the time goes in v1:
time: 125 us; the launch traced here: 124 us
  Pallas kernels  59.7 us (48%)
  matrix products  39.8 us (32%)
  local copies, waits for them, and re-layouts  11.8 us (9%)
  blocking collectives  10.4 us (8%)
  other arithmetic  1.39 us (1%)
    pallas_call x2, Pallas kernels, exchange(): pl.pallas_call(functools.partial(exchange_kernel, groups, shards), out_sh...  42.7 us
    pallas_call x1, Pallas kernels, total_over_mesh(): pl.pallas_call(functools.partial(total_kernel, groups, shards), out_shape...  17.1 us
    dot_general x1, matrix products, on_device(): jnp.einsum('eif,eid->efd', hidden_low, grad_slots_out, preferred_element_...  7.01 us
    dot_general x1, matrix products, on_device(): jnp.einsum('eid,eif->edf', slot_inputs, grad_pre, preferred_element_type=...  6.72 us
    dot_general x1, matrix products, on_device(): jnp.einsum('eid,efd->eif', grad_slots_out, w_out, preferred_element_type=...  6.19 us
    dot_general x1, matrix products, on_device(): jnp.einsum('eid,edf->eif', slot_inputs, w_in, preferred_element_type=wide)  5.68 us
    all_gather x1, blocking collectives, dispatch_softmax(): both = lax.all_gather(jnp.stack([local_max, local_sum]), 'tensor')  5.29 us
    psum x1, blocking collectives, on_device(): column_dot = lax.psum(jnp.sum(grad_dispatch * dispatch, axis=1), 'tensor')  5.11 us

profile of v1, /device:TPU:0, one launch (start us, length us, event | category | flops | bytes accessed | tf_op | source)
XLA Modules:
  0.0 124.1 jit_solution(3255603323347701572)
XLA Ops:
  0.6 1.1 copy-done
  1.7 1.3 %fusion.35 = (f32[4,32]{1,0:T(4,128)S(1)}, f32[4,72,32]{1,2,0:T(8,128)S(1)}) fusion(bf16[4,72,1024]{2,1,0:T(8,128)(2,1)S(1)} %copy-done, bf16[1024,32]{0,1:T(8,128)(2,1)} %param.7), kind=kOutput, calls=%fused_computation.59 | convolution fusion | flops 18883456 | bytes 692736 | tf_op jit(solution)/shard_map/isd,de->ise/dot_general | solution.py:262
  3.0 0.2 exponential_reduce_fusion
  3.2 5.3 %all-gather = f32[4,4,32]{2,1,0:T(4,128)S(1)} all-gather(f32[2,4,32]{2,1,0:T(4,128)S(1)} %pad_maximum_fusion), channel_id=2, replica_groups=mesh['dp'=16,'tensor'=2] {'tensor'}, dimensions={0}, use_global_device_ids=true | all-gather | bytes 3072 | tf_op jit(solution)/shard_map/all_gather | solution.py:254
  8.5 0.2 fusion.34
  8.7 1.3 %convolution_convert_fusion.4 = bf16[4,32,1024]{2,1,0:T(8,128)(2,1)S(1)} fusion(bf16[4,72,1024]{2,1,0:T(8,128)(2,1)} %param.6, f32[4,72]{1,0:T(4,128)S(1)} %get-tuple-element.8, f32[4,72,32]{1,2,0:T(8,128)S(1)} %get-tuple-element.11), kind=kOutput, calls=%fused_computation.10 | convolution fusion | flops 19033408 | bytes 889984 | tf_op jit(solution)/shard_map/ise,isd->ied/dot_general | solution.py:270
  10.0 0.2 stack.31
  10.2 0.2 copy.20
  10.4 0.3 convolution_convert_fusion.5
  10.7 0.2 stack.30
  10.9 0.2 copy.19
  11.1 0.3 maximum_bitcast_fusion
  11.5 0.9 reshape.54.x_ref
  12.4 22.5 %exchange_0.1 = bf16[2,16,16,512]{3,2,1,0:T(8,128)(2,1)} custom-call(bf16[2,16,16,512]{3,2,1,0:T(8,128)(2,1)} %reshape.54.x_ref), custom_call_target="tpu_custom_call" | custom-call | tf_op jit(solution)/shard_map/exchange_0/pallas_call | solution.py:120
  34.8 1.2 reshape.55
  36.0 0.2 fusion.33
  36.2 0.3 copy.22
  36.5 0.2 squeeze.22
  36.7 0.3 copy.21
  37.0 0.2 squeeze.21
  37.2 6.2 %fusion.36 = f32[2,64,2048]{2,1,0:T(8,128)S(1)} fusion(bf16[2,64,1024]{2,1,0:T(8,128)(2,1)S(1)} %squeeze.22, bf16[2,2048,1024]{2,1,0:T(8,128)(2,1)} %param.9), kind=kOutput, calls=%fused_computation.60 | convolution fusion | flops 536870912 | bytes 9699328 | tf_op jit(solution)/shard_map/eid,efd->eif/dot_general | solution.py:277
  43.4 5.7 %fusion.16 = (bf16[2,64,2048]{2,1,0:T(8,128)(2,1)S(1)}, f32[2,64,2048]{2,1,0:T(8,128)S(1)}) fusion(f32[2,64,2048]{2,1,0:T(8,128)S(1)} %fusion.36, bf16[2,64,1024]{2,1,0:T(8,128)(2,1)S(1)} %squeeze.21, bf16[2,1024,2048]{2,1,0:T(8,128)(2,1)} %param.8), kind=kOutput, calls=%fused_computation.28 | convolution fusion | flops 542113792 | bytes 11272192 | tf_op jit(solution)/shard_map/eid,edf->eif/dot_general | solution.py:274
  49.1 2.7 %convolution_convert_fusion.2 = bf16[2,64,1024]{2,1,0:T(8,128)(2,1)S(1)} fusion(bf16[2,64,2048]{2,1,0:T(8,128)(2,1)S(1)} %get-tuple-element.12, bf16[2,1024,2048]{2,1,0:T(8,128)(2,1)S(1)} %bitcast.72), kind=kOutput, calls=%fused_computation.8 | convolution fusion | flops 537001984 | bytes 9175040 | tf_op jit(solution)/shard_map/eif,edf->eid/dot_general | solution.py:282
  51.8 0.2 stack.34
  52.0 0.3 copy.24
  52.2 4.9 %convolution_convert_fusion.3 = bf16[2,64,1024]{2,1,0:T(8,128)(2,1)S(1)} fusion(bf16[2,2048,1024]{2,1,0:T(8,128)(2,1)} %param.9, f32[2,64,2048]{2,1,0:T(8,128)S(1)} %get-tuple-element.13), kind=kOutput, calls=%fused_computation.9 | convolution fusion | flops 539361280 | bytes 9699328 | tf_op jit(solution)/shard_map/eif,efd->eid/dot_general | solution.py:281
  57.2 0.2 stack.33
  57.4 0.3 copy.23
  57.7 0.7 maximum_bitcast_fusion.1
  58.4 1.0 reshape.56.x_ref
  59.4 20.2 %exchange_1.1 = bf16[2,16,16,512]{3,2,1,0:T(8,128)(2,1)} custom-call(bf16[2,16,16,512]{3,2,1,0:T(8,128)(2,1)} %reshape.56.x_ref), custom_call_target="tpu_custom_call" | custom-call | tf_op jit(solution)/shard_map/exchange_1/pallas_call | solution.py:120
  79.6 1.2 reshape.57
  80.8 0.4 fusion.32
  81.2 0.3 copy.25
  81.5 0.2 squeeze.23
  81.7 0.4 multiply_reduce_fusion.1
  82.1 5.1 %psum.7 = f32[4,32]{1,0:T(4,128)S(1)} all-reduce(f32[4,32]{1,0:T(4,128)S(1)} %get-tuple-element.14), channel_id=1, replica_groups=mesh['dp'=16,'tensor'=2] {'tensor'}, use_global_device_ids=true, to_apply=%region_8.0 | all-reduce | flops 128 | bytes 1024 | tf_op jit(solution)/shard_map/psum | solution.py:294
  87.2 0.3 copy.26
  87.5 0.2 squeeze.24
  87.6 0.3 convolution_bitcast_fusion.2
  87.9 0.3 convolution_bitcast_fusion
  88.3 0.7 copy.28
  89.0 17.1 %router_total.1 = f32[32,8,128]{2,1,0:T(8,128)} custom-call(f32[32,8,128]{2,1,0:T(8,128)} %bitcast.75), custom_call_target="tpu_custom_call" | custom-call | tf_op jit(solution)/shard_map/router_total/pallas_call | solution.py:209
  106.1 1.6 %copy.31 = f32[4,8,8,128]{3,1,2,0:T(8,128)} copy(f32[4,8,8,128]{3,2,1,0:T(8,128)} %bitcast.76) | data formatting | bytes 262144
  107.7 1.4 %fusion.9 = f32[4,72,1024]{2,1,0:T(8,128)S(1)} fusion(f32[4,72,32]{1,2,0:T(8,128)} %copy-done.6, bf16[1024,32]{0,1:T(8,128)(2,1)S(1)} %copy-done.4, f32[4,72,32]{1,2,0:T(8,128)} %copy-done.5, f32[4,32]{1,0:T(4,128)S(1)} %psum.7, f32[4,72,32]{1,2,0:T(8,128)} %copy-done.7, f32[4,72]{1,0:T(4,128)S(1)} %get-tuple-element.8, ...), kind=kOutput, calls=%fused_computation.21 | convolution fusion | flops 18976064 | bytes 1395328 | tf_op jit(solution)/shard_map/ise,de->isd/dot_general | solution.py:302
  109.1 1.3 %fusion.2 = bf16[4,72,1024]{2,1,0:T(8,128)(2,1)} fusion(f32[4,72,1024]{2,1,0:T(8,128)S(1)} %fusion.9, bf16[4,32,1024]{2,1,0:T(8,128)(2,1)S(1)} %squeeze.23, f32[4,72,32]{1,2,0:T(8,128)S(1)} %get-tuple-element.11, f32[4,32]{1,0:T(4,128)S(1)} %fusion.28, f32[4,32]{1,0:T(4,128)S(1)} %bitcast_reduce_fusion), kind=kOutput, calls=%fused_computation.7 | convolution fusion | flops 19491840 | bytes 2069504 | tf_op jit(solution)/shard_map/ise,ied->isd/dot_general | solution.py:299
  110.3 7.0 %convolution_convert_fusion = bf16[2,2048,1024]{2,1,0:T(8,128)(2,1)} fusion(bf16[2,64,1024]{2,1,0:T(8,128)(2,1)S(1)} %squeeze.22, f32[2,64,2048]{2,1,0:T(8,128)} %copy-done.2), kind=kOutput, calls=%fused_computation.2 | convolution fusion | flops 543424512 | bytes 9699328 | tf_op jit(solution)/shard_map/eif,eid->efd/dot_general | solution.py:286
  117.4 6.7 %convolution_convert_fusion.1 = bf16[2,1024,2048]{2,1,0:T(8,128)(2,1)} fusion(bf16[2,64,1024]{2,1,0:T(8,128)(2,1)} %copy-done.3, bf16[2,64,2048]{2,1,0:T(8,128)(2,1)S(1)} %get-tuple-element.12), kind=kOutput, calls=%fused_computation.3 | convolution fusion | flops 541065216 | bytes 9175040 | tf_op jit(solution)/shard_map/eid,eif->edf/dot_general | solution.py:289
  (23 shorter events, 0.1 us)
Async XLA Ops:
  0.6 1.1 copy-start
  8.7 79.3 %copy-start.7 = (f32[4,72,32]{1,2,0:T(8,128)}, f32[4,72,32]{1,2,0:T(8,128)S(1)}, u32[]{:S(2)}) copy-start(f32[4,72,32]{1,2,0:T(8,128)S(1)} %get-tuple-element.9) | copy-start | bytes 110596
  37.1 11.9 %copy-start.3 = (bf16[2,64,1024]{2,1,0:T(8,128)(2,1)}, bf16[2,64,1024]{2,1,0:T(8,128)(2,1)S(1)}, u32[]{:S(2)}) copy-start(bf16[2,64,1024]{2,1,0:T(8,128)(2,1)S(1)} %squeeze.21) | copy-start | bytes 786436
  37.1 11.9 %slice-start = ((s8[8388608]{0:T(1024)(128)(4,1)}), s8[4194304]{0:T(1024)(128)(4,1)S(1)}, s32[]{:S(2)}) async-start(s8[8388608]{0:T(1024)(128)(4,1)} %bitcast.71), calls=%async_computation | async-start | bytes 8388608
  43.3 5.7 %slice-start.1 = ((s8[8388608]{0:T(1024)(128)(4,1)}), s8[4194304]{0:T(1024)(128)(4,1)S(1)}, s32[]{:S(2)}) async-start(s8[8388608]{0:T(1024)(128)(4,1)} %bitcast.71), calls=%async_computation.1 | async-start | bytes 8388608
  49.1 3.2 %copy-start.2 = (f32[2,64,2048]{2,1,0:T(8,128)}, f32[2,64,2048]{2,1,0:T(8,128)S(1)}, u32[]{:S(2)}) copy-start(f32[2,64,2048]{2,1,0:T(8,128)S(1)} %get-tuple-element.13) | copy-start | bytes 3145732
  57.2 30.4 %copy-start.1 = (bf16[4,72,1024]{2,1,0:T(8,128)(2,1)S(1)}, bf16[4,72,1024]{2,1,0:T(8,128)(2,1)}, u32[]{:S(2)}) copy-start(bf16[4,72,1024]{2,1,0:T(8,128)(2,1)} %param.6) | copy-start | bytes 1769476
  57.2 50.5 %copy-start.4 = (bf16[1024,32]{0,1:T(8,128)(2,1)S(1)}, bf16[1024,32]{0,1:T(8,128)(2,1)}, u32[]{:S(2)}) copy-start(bf16[1024,32]{0,1:T(8,128)(2,1)} %param.7) | copy-start | bytes 196612
  82.1 25.6 %copy-start.5 = (f32[4,72,32]{1,2,0:T(8,128)}, f32[4,72,32]{1,2,0:T(8,128)S(1)}, u32[]{:S(2)}) copy-start(f32[4,72,32]{1,2,0:T(8,128)S(1)} %get-tuple-element.15) | copy-start | bytes 110596
  87.9 19.7 %copy-start.6 = (f32[4,72,32]{1,2,0:T(8,128)}, f32[4,72,32]{1,2,0:T(8,128)S(1)}, u32[]{:S(2)}) copy-start(f32[4,72,32]{1,2,0:T(8,128)S(1)} %convolution_bitcast_fusion.2) | copy-start | bytes 110596

commit v2 on v1

--- a/solution.py
+++ b/solution.py
@@ -8,6 +8,7 @@
 from jax.sharding import PartitionSpec as P
 
 MESH = pl.DeviceIdType.MESH
+WAIT_COST = pl.CostEstimate(flops=18_000_000_000, bytes_accessed=50_000_000, transcendentals=0)
 
 
 def exchange_kernel(
@@ -111,6 +112,10 @@
         return carry
 
     lax.fori_loop(1, groups, finish_far, 0)
+
+
+def grant(x, copies):
+    return copies * x.size * x.dtype.itemsize + 2**20
 
 
 def exchange(x, collective_id):
@@ -132,7 +137,10 @@
             pltpu.SemaphoreType.DMA(near_shape),
             pltpu.SemaphoreType.DMA(near_shape),
         ],
-        compiler_params=pltpu.CompilerParams(collective_id=collective_id, has_side_effects=True),
+        compiler_params=pltpu.CompilerParams(
+            collective_id=collective_id, has_side_effects=True, vmem_limit_bytes=grant(x, 6)
+        ),
+        cost_estimate=WAIT_COST,
         name=f"exchange_{collective_id}",
     )(x)
 
@@ -204,7 +212,10 @@
 
 def total_over_mesh(x, groups, shards, collective_id):
     devices = groups * shards
-    blocks = x.reshape(devices, -1, 128)
+    experts, width = x.shape
+    rows = experts * width // (devices * 128)
+    blocks = x.reshape(experts // rows, rows, width // 128, 128).transpose(0, 2, 1, 3)
+    blocks = blocks.reshape(devices, rows, 128)
     vmem = pl.BlockSpec(memory_space=pltpu.VMEM)
     out = pl.pallas_call(
         functools.partial(total_kernel, groups, shards),
@@ -218,10 +229,40 @@
             pltpu.SemaphoreType.DMA((devices,)),
             pltpu.SemaphoreType.DMA((devices,)),
         ],
-        compiler_params=pltpu.CompilerParams(collective_id=collective_id, has_side_effects=True),
+        compiler_params=pltpu.CompilerParams(
+            collective_id=collective_id, has_side_effects=True, vmem_limit_bytes=grant(blocks, 6)
+        ),
+        cost_estimate=WAIT_COST,
         name="router_total",
     )(blocks)
+    out = out.reshape(experts // rows, width // 128, rows, 128).transpose(0, 2, 1, 3)
     return out.reshape(x.shape)
+
+
+def outer_kernel(a_ref, b_ref, out_ref):
+    out_ref[0] = lax.dot_general(
+        a_ref[0], b_ref[0], (((0,), (0,)), ((), ())), preferred_element_type=jnp.float32
+    ).astype(out_ref.dtype)
+
+
+def outer_sums(a, b, tile):
+    experts, images, m = a.shape
+    n = b.shape[2]
+    return pl.pallas_call(
+        outer_kernel,
+        grid=(experts, m // tile),
+        in_specs=[
+            pl.BlockSpec((1, images, tile), lambda e, k: (e, 0, k)),
+            pl.BlockSpec((1, images, n), lambda e, k: (e, 0, 0)),
+        ],
+        out_specs=pl.BlockSpec((1, tile, n), lambda e, k: (e, k, 0)),
+        out_shape=jax.ShapeDtypeStruct((experts, m, n), a.dtype),
+        compiler_params=pltpu.CompilerParams(vmem_limit_bytes=12 * 2**20),
+        cost_estimate=pl.CostEstimate(
+            flops=2 * experts * images * m * n, bytes_accessed=2 * experts * m * n, transcendentals=0
+        ),
+        name="outer_sums",
+    )(a, b)
 
 
 def to_experts(rows, groups, shards, collective_id):
@@ -283,12 +324,8 @@
         ],
         groups, shards, 1,
     )
-    grad_w_out = jnp.einsum(
-        "eif,eid->efd", hidden_low, grad_slots_out, preferred_element_type=wide
-    ).astype(jnp.bfloat16)
-    grad_w_in = jnp.einsum(
-        "eid,eif->edf", slot_inputs, grad_pre, preferred_element_type=wide
-    ).astype(jnp.bfloat16)
+    grad_w_out = outer_sums(hidden_low, grad_slots_out, min(512, hidden_low.shape[2]))
+    grad_w_in = outer_sums(slot_inputs, grad_pre, min(256, slot_inputs.shape[2]))
     grad_combine = jnp.einsum("isd,ied->ise", cotangent, slot_outputs, preferred_element_type=wide)
     grad_dispatch = jnp.einsum("isd,ied->ise", tokens, grad_slots_in, preferred_element_type=wide)
     column_dot = lax.psum(jnp.sum(grad_dispatch * dispatch, axis=1), "tensor")

time: 125 us -> 117 us (0.936)
  matrix products: 39.8 us -> 29.1 us
  Pallas kernels: 59.7 us -> 67.6 us
  local copies, waits for them, and re-layouts: 11.8 us -> 6.61 us
    dot_general x2 -> x0, matrix products: 13.7 us -> none  [the longest x1 7.01 us: on_device(): jnp.einsum('eif,eid->efd', hidden_low, grad_slots_out, preferred_element_...]
    pallas_call x0 -> x2, Pallas kernels: none -> 12.4 us  [outer_sums(): pl.pallas_call(outer_kernel, grid=(experts, m // tile), in_specs=[pl.Bloc...]
    dot_general x1, matrix products: 2.66 us -> 6.04 us  [on_device(): jnp.einsum('eif,edf->eid', grad_pre, w_in, preferred_element_type=wide)]
    dot_general x1, matrix products: 4.94 us -> 1.6 us  [on_device(): jnp.einsum('eif,efd->eid', hidden_low, w_out, preferred_element_type=wide)]
    pallas_call x2, Pallas kernels: 42.7 us -> 39.5 us  [exchange(): pl.pallas_call(functools.partial(exchange_kernel, groups, shards), out_sh...]
    unnamed x22 -> x13, local copies, waits for them, and re-layouts: 3.42 us -> 1.75 us
    pallas_call x1, Pallas kernels: 17.1 us -> 15.7 us  [total_over_mesh(): pl.pallas_call(functools.partial(total_kernel, groups, shards), out_shape...]
where the time goes in v2:
time: 117 us; the launch traced here: 116 us
  Pallas kernels  67.6 us (58%)
  matrix products  29.1 us (25%)
  blocking collectives  10.2 us (9%)
  local copies, waits for them, and re-layouts  6.61 us (6%)
  other arithmetic  1.91 us (2%)
    pallas_call x2, Pallas kernels, exchange(): pl.pallas_call(functools.partial(exchange_kernel, groups, shards), out_sh...  39.5 us
    pallas_call x1, Pallas kernels, total_over_mesh(): pl.pallas_call(functools.partial(total_kernel, groups, shards), out_shape...  15.7 us
    pallas_call x2, Pallas kernels, outer_sums(): pl.pallas_call(outer_kernel, grid=(experts, m // tile), in_specs=[pl.Bloc...  12.4 us
    dot_general x1, matrix products, on_device(): jnp.einsum('eid,efd->eif', grad_slots_out, w_out, preferred_element_type=...  6.19 us
    dot_general x1, matrix products, on_device(): jnp.einsum('eif,edf->eid', grad_pre, w_in, preferred_element_type=wide)  6.04 us
    dot_general x1, matrix products, on_device(): jnp.einsum('eid,edf->eif', slot_inputs, w_in, preferred_element_type=wide)  5.74 us
    all_gather x1, blocking collectives, dispatch_softmax(): both = lax.all_gather(jnp.stack([local_max, local_sum]), 'tensor')  5.29 us
    psum x1, blocking collectives, on_device(): column_dot = lax.psum(jnp.sum(grad_dispatch * dispatch, axis=1), 'tensor')  4.93 us

profile of v2, /device:TPU:0, one launch (start us, length us, event | category | flops | bytes accessed | tf_op | source)
XLA Modules:
  0.0 116.3 jit_solution(18331750805503178463)
XLA Ops:
  0.6 0.0 copy-start
  0.6 1.1 copy-done
  1.7 1.3 %fusion.36 = (f32[4,32]{1,0:T(4,128)S(1)}, f32[4,72,32]{1,2,0:T(8,128)S(1)}) fusion(bf16[4,72,1024]{2,1,0:T(8,128)(2,1)S(1)} %copy-done, bf16[1024,32]{0,1:T(8,128)(2,1)} %param.7), kind=kOutput, calls=%fused_computation.57 | convolution fusion | flops 18883456 | bytes 692736 | tf_op jit(solution)/shard_map/isd,de->ise/dot_general | solution.py:303
  3.0 0.2 exponential_reduce_fusion
  3.2 5.3 %all-gather = f32[4,4,32]{2,1,0:T(4,128)S(1)} all-gather(f32[2,4,32]{2,1,0:T(4,128)S(1)} %pad_maximum_fusion), channel_id=2, replica_groups=mesh['dp'=16,'tensor'=2] {'tensor'}, dimensions={0}, use_global_device_ids=true | all-gather | bytes 3072 | tf_op jit(solution)/shard_map/all_gather | solution.py:295
  8.5 0.7 fusion.35
  9.2 1.3 %convolution_convert_fusion.2 = bf16[4,32,1024]{2,1,0:T(8,128)(2,1)S(1)} fusion(bf16[4,72,1024]{2,1,0:T(8,128)(2,1)} %param.6, f32[4,72]{1,0:T(4,128)S(1)} %get-tuple-element.10, f32[4,72,32]{1,2,0:T(8,128)S(1)} %get-tuple-element.13), kind=kOutput, calls=%fused_computation.8 | convolution fusion | flops 19033408 | bytes 889984 | tf_op jit(solution)/shard_map/ise,isd->ied/dot_general | solution.py:311
  10.5 0.2 stack.31
  10.7 0.2 copy.19
  10.9 0.3 convolution_convert_fusion.3
  11.2 0.2 stack.30
  11.4 0.2 copy.18
  11.6 0.3 maximum_bitcast_fusion
  11.9 0.1 reshape.60.x_ref
  12.1 20.7 %exchange_0.1 = bf16[2,16,16,512]{3,2,1,0:T(8,128)(2,1)S(1)} custom-call(bf16[2,16,16,512]{3,2,1,0:T(8,128)(2,1)S(1)} %reshape.60.x_ref), custom_call_target="tpu_custom_call" | custom-call | flops 17999998976 | bytes 50000000 | tf_op jit(solution)/shard_map/exchange_0/pallas_call | solution.py:125
  32.8 0.1 reshape.61
  32.9 0.5 copy.27
  33.5 0.4 fusion.34
  33.9 0.2 squeeze.22.b_ref
  34.0 0.2 squeeze.21.a_ref
  34.2 0.0 slice-start
  34.2 6.2 %fusion.37 = f32[2,64,2048]{2,1,0:T(8,128)S(1)} fusion(bf16[2,64,1024]{2,1,0:T(8,128)(2,1)S(1)} %squeeze.22.b_ref, bf16[2,2048,1024]{2,1,0:T(8,128)(2,1)} %param.9), kind=kOutput, calls=%fused_computation.58 | convolution fusion | flops 536870912 | bytes 9699328 | tf_op jit(solution)/shard_map/eid,efd->eif/dot_general | solution.py:318
  40.4 5.7 %multiply_convert_fusion = (bf16[2,64,2048]{2,1,0:T(8,128)(2,1)S(1)}, bf16[2,64,2048]{2,1,0:T(8,128)(2,1)S(1)}) fusion(f32[2,64,2048]{2,1,0:T(8,128)S(1)} %fusion.37, bf16[2,64,1024]{2,1,0:T(8,128)(2,1)S(1)} %squeeze.21.a_ref, bf16[2,1024,2048]{2,1,0:T(8,128)(2,1)} %param.8), kind=kOutput, calls=%fused_computation.27 | convolution fusion | flops 542638080 | bytes 10747904 | tf_op jit(solution)/shard_map/eid,edf->eif/dot_general | solution.py:315
  46.2 1.6 %convolution_convert_fusion.1 = bf16[2,64,1024]{2,1,0:T(8,128)(2,1)S(1)} fusion(bf16[2,64,2048]{2,1,0:T(8,128)(2,1)S(1)} %get-tuple-element.4.a_ref, bf16[2,2048,1024]{2,1,0:T(8,128)(2,1)S(1)} %bitcast.77), kind=kOutput, calls=%fused_computation.7 | convolution fusion | flops 537001984 | bytes 9175040 | tf_op jit(solution)/shard_map/eif,efd->eid/dot_general | solution.py:322
  47.8 0.2 stack.33
  48.0 0.3 copy.21
  48.3 6.0 %convolution_convert_fusion = bf16[2,64,1024]{2,1,0:T(8,128)(2,1)S(1)} fusion(bf16[2,64,2048]{2,1,0:T(8,128)(2,1)S(1)} %get-tuple-element.5.b_ref, bf16[2,1024,2048]{2,1,0:T(8,128)(2,1)} %param.8), kind=kOutput, calls=%fused_computation.6 | convolution fusion | flops 537001984 | bytes 9175040 | tf_op jit(solution)/shard_map/eif,edf->eid/dot_general | solution.py:323
  54.3 0.2 stack.34
  54.5 0.3 copy.22
  54.8 0.7 maximum_bitcast_fusion.1
  55.5 0.2 reshape.62.x_ref
  55.7 18.8 %exchange_1.1 = bf16[2,16,16,512]{3,2,1,0:T(8,128)(2,1)S(1)} custom-call(bf16[2,16,16,512]{3,2,1,0:T(8,128)(2,1)S(1)} %reshape.62.x_ref), custom_call_target="tpu_custom_call" | custom-call | flops 17999998976 | bytes 50000000 | tf_op jit(solution)/shard_map/exchange_1/pallas_call | solution.py:125
  74.4 0.2 reshape.63
  74.6 0.4 fusion.33
  75.0 0.3 copy.23
  75.3 0.2 squeeze.23
  75.5 0.4 multiply_reduce_fusion.1
  75.9 4.9 %psum.7 = f32[4,32]{1,0:T(4,128)S(1)} all-reduce(f32[4,32]{1,0:T(4,128)S(1)} %get-tuple-element.14), channel_id=1, replica_groups=mesh['dp'=16,'tensor'=2] {'tensor'}, use_global_device_ids=true, to_apply=%region_8.0 | all-reduce | flops 128 | bytes 1024 | tf_op jit(solution)/shard_map/psum | solution.py:331
  80.8 0.3 copy.24
  81.1 0.2 squeeze.24
  81.3 1.3 %convolution_bitcast_fusion.1 = f32[4,72,32]{1,2,0:T(8,128)S(1)} fusion(bf16[4,32,1024]{2,1,0:T(8,128)(2,1)S(1)} %squeeze.24, bf16[4,72,1024]{2,1,0:T(8,128)(2,1)} %param.6), kind=kOutput, calls=%fused_computation.16 | convolution fusion | flops 18874368 | bytes 888832 | tf_op jit(solution)/shard_map/isd,ied->ise/dot_general | solution.py:329
  82.6 1.3 %fusion.9 = f32[32,1024,1]{1,0,2:T(8,128)S(1)} fusion(bf16[4,72,1024]{2,1,0:T(8,128)(2,1)S(1)} %copy-done, f32[4,72,32]{1,2,0:T(8,128)S(1)} %convolution_bitcast_fusion.1, f32[4,72,32]{1,2,0:T(8,128)S(1)} %get-tuple-element.15, f32[4,32]{1,0:T(4,128)S(1)} %psum.7, f32[4,72,32]{1,2,0:T(8,128)} %get-tuple-element.11, f32[4,72]{1,0:T(4,128)S(1)} %get-tuple-element.10, ...), kind=kOutput, calls=%fused_computation.18 | convolution fusion | flops 18976064 | bytes 871040 | tf_op jit(solution)/shard_map/isd,ise->ed/dot_general | solution.py:343
  83.9 15.7 %router_total.1 = f32[32,8,128]{2,1,0:T(8,128)S(1)} custom-call(f32[32,8,128]{2,1,0:T(8,128)S(1)} %bitcast.75), custom_call_target="tpu_custom_call" | custom-call | flops 17999998976 | bytes 50000000 | tf_op jit(solution)/shard_map/router_total/pallas_call | solution.py:220
  99.6 1.5 %fusion.10 = f32[4,72,1024]{2,1,0:T(8,128)S(1)} fusion(f32[4,72,32]{1,2,0:T(8,128)} %copy-done.3, bf16[1024,32]{0,1:T(8,128)(2,1)} %param.7, f32[4,72,32]{1,2,0:T(8,128)} %copy-done.2, f32[4,32]{1,0:T(4,128)S(1)} %psum.7, f32[4,72,32]{1,2,0:T(8,128)} %get-tuple-element.11, f32[4,72]{1,0:T(4,128)S(1)} %get-tuple-element.10, ...), kind=kOutput, calls=%fused_computation.19 | convolution fusion | flops 18976064 | bytes 1395328 | tf_op jit(solution)/shard_map/ise,de->isd/dot_general | solution.py:339
  101.1 2.2 %fusion.2 = bf16[4,72,1024]{2,1,0:T(8,128)(2,1)} fusion(f32[4,72,1024]{2,1,0:T(8,128)S(1)} %fusion.10, bf16[4,32,1024]{2,1,0:T(8,128)(2,1)} %copy-done.1, f32[4,72,32]{1,2,0:T(8,128)S(1)} %get-tuple-element.13, f32[4,32]{1,0:T(4,128)S(1)} %fusion.29, f32[4,32]{1,0:T(4,128)S(1)} %bitcast_reduce_fusion), kind=kOutput, calls=%fused_computation.5 | convolution fusion | flops 19491840 | bytes 2069504 | tf_op jit(solution)/shard_map/ise,ied->isd/dot_general | solution.py:336
  103.3 6.2 %outer_sums.2 = bf16[2,1024,2048]{2,1,0:T(8,128)(2,1)} custom-call(bf16[2,64,1024]{2,1,0:T(8,128)(2,1)S(1)} %squeeze.21.a_ref, bf16[2,64,2048]{2,1,0:T(8,128)(2,1)S(1)} %get-tuple-element.5.b_ref), custom_call_target="tpu_custom_call" | custom-call | flops 536870912 | bytes 8388608 | tf_op jit(solution)/shard_map/outer_sums/pallas_call | solution.py:251
  109.5 6.2 %outer_sums.3 = bf16[2,2048,1024]{2,1,0:T(8,128)(2,1)} custom-call(bf16[2,64,2048]{2,1,0:T(8,128)(2,1)S(1)} %get-tuple-element.4.a_ref, bf16[2,64,1024]{2,1,0:T(8,128)(2,1)S(1)} %squeeze.22.b_ref), custom_call_target="tpu_custom_call" | custom-call | flops 536870912 | bytes 8388608 | tf_op jit(solution)/shard_map/outer_sums/pallas_call | solution.py:251
  115.7 0.7 copy.29
  (13 shorter events, 0.1 us)
Async XLA Ops:
  0.6 1.1 copy-start
  34.2 12.0 %slice-start = ((s8[8388608]{0:T(1024)(128)(4,1)}), s8[4194304]{0:T(1024)(128)(4,1)S(1)}, s32[]{:S(2)}) async-start(s8[8388608]{0:T(1024)(128)(4,1)} %bitcast.76), calls=%async_computation | async-start | bytes 8388608
  40.4 5.8 %slice-start.1 = ((s8[8388608]{0:T(1024)(128)(4,1)}), s8[4194304]{0:T(1024)(128)(4,1)S(1)}, s32[]{:S(2)}) async-start(s8[8388608]{0:T(1024)(128)(4,1)} %bitcast.76), calls=%async_computation.1 | async-start | bytes 8388608
  75.5 5.8 %copy-start.1 = (bf16[4,32,1024]{2,1,0:T(8,128)(2,1)}, bf16[4,32,1024]{2,1,0:T(8,128)(2,1)S(1)}, u32[]{:S(2)}) copy-start(bf16[4,32,1024]{2,1,0:T(8,128)(2,1)S(1)} %squeeze.23) | copy-start | bytes 786436
  75.9 23.7 %copy-start.2 = (f32[4,72,32]{1,2,0:T(8,128)}, f32[4,72,32]{1,2,0:T(8,128)S(1)}, u32[]{:S(2)}) copy-start(f32[4,72,32]{1,2,0:T(8,128)S(1)} %get-tuple-element.15) | copy-start | bytes 110596
  82.6 17.0 %copy-start.3 = (f32[4,72,32]{1,2,0:T(8,128)}, f32[4,72,32]{1,2,0:T(8,128)S(1)}, u32[]{:S(2)}) copy-start(f32[4,72,32]{1,2,0:T(8,128)S(1)} %convolution_bitcast_fusion.1) | copy-start | bytes 110596
